TPU v7x, 32 devices: a whole 2x2x4 slice. The times are simulated.
32 devices in a mesh: grp: 8 (over z, x), sub: 4 (over y, core).
Axes of the slice: x: 2, y: 2, z: 4, core: 2. Of those that a mesh axis runs over, the one named last changes fastest.
Arguments:
- child_moments: bfloat16 [294, 32768], P(None, ('grp', 'sub')), may hold values from -6 to 6
- upward_matrix: bfloat16 [294, 8, 294], replicated, may hold values from -0.125 to 0.125
- project_matrix: bfloat16 [64, 294], replicated, may hold values from -0.375 to 0.375
- transfer_matrix: bfloat16 [64, 20224], replicated, may hold values from -0.0546875 to 0.0546875
- expand_matrix: bfloat16 [294, 64], replicated, may hold values from -0.75 to 0.75
- downward_matrix: bfloat16 [294, 8, 294], replicated, may hold values from -0.375 to 0.375
- neighbour_list: int32 [316, 4096], P(None, ('grp', 'sub')), may hold values from 0 to 832, as said below
- ghost_map: int32 [32, 80], P(('grp', 'sub')), may hold values from 0 to 128, as said below
Outputs:
- child_locals: bfloat16 [294, 32768], P(None, ('grp', 'sub'))
Inputs may be any that keep to these rules, and one draw needn't show every extreme that they name: `neighbour_list`: entries below 832 name a source slot; each column has between 95 and 189 such entries, and the first column of every device's block has exactly 189. Every ghost slot that is named holds a box. `ghost_map`: the groups stand in a three-dimensional arrangement; a device sends boxes only to groups next to its own there (all other destinations hold 128 only). Slot 0 of every such destination names a box, and every device fills all 10 slots of at least one destination.
All inputs are finite; a program needn't handle non-finite values.
Results may differ from a plain program's by a relative error of at most 0.0085.
Values may be sent and summed in bfloat16 or wider, within the bound.
No kernel may reach another device: no remote copies, remote signals or barrier semaphores. Data moves between devices by JAX's collectives and lax.ppermute only.
A program may use at most 64 MiB of HBM per device.

v0:
```python
import jax
import jax.numpy as jnp
from jax import lax
from jax.sharding import PartitionSpec as P


def on_device(
    child_moments,
    upward_matrix,
    project_matrix,
    transfer_matrix,
    expand_matrix,
    downward_matrix,
    neighbour_list,
    ghost_map,
):
    surface = child_moments.shape[0]
    box_count = child_moments.shape[1] // 8
    coeff_rows = project_matrix.shape[0]
    children = child_moments.reshape(surface, 8, box_count)
    parent = jnp.einsum(
        "icj,jcb->ib", upward_matrix, children, preferred_element_type=jnp.float32
    ).astype(jnp.bfloat16)
    packed_rows = lax.dot_general(
        parent, project_matrix, (((0,), (1,)), ((), ())), preferred_element_type=jnp.float32
    ).astype(jnp.bfloat16)
    slot_ids = ghost_map.reshape(-1)
    source = jnp.concatenate([packed_rows, jnp.zeros((1, coeff_rows), jnp.bfloat16)], axis=0)[
        slot_ids
    ]
    ghosts = lax.all_to_all(source, "grp", split_axis=0, concat_axis=0, tiled=True)
    mine = jnp.concatenate([packed_rows, ghosts], axis=0)
    sub_count = lax.axis_size("sub")
    ghost_width = ghosts.shape[0]
    width = box_count + ghost_width
    group_boxes = sub_count * box_count
    pool_size = sub_count * width
    lists = jnp.transpose(neighbour_list)
    ghost_index = lists - group_boxes
    own_place = lists // box_count * width + lists % box_count
    ghost_place = ghost_index // ghost_width * width + box_count + ghost_index % ghost_width
    remap = jnp.where(lists < group_boxes, own_place, ghost_place)
    remap = jnp.where(lists < pool_size, remap, -1)
    whole_pool = lax.all_gather(mine, "sub", axis=0, tiled=True)
    span = whole_pool.shape[0]
    local = remap - 0
    valid = (local >= 0) & (local < span)
    index = jnp.where(valid, local, span)
    extended = jnp.concatenate([whole_pool, jnp.zeros((1, coeff_rows), jnp.bfloat16)], axis=0)
    picked = extended[index].reshape(box_count, -1)
    local_float = lax.dot_general(
        picked, transfer_matrix, (((1,), (1,)), ((), ())), preferred_element_type=jnp.float32
    )
    local_coeff = local_float.astype(jnp.bfloat16)
    local_moment = lax.dot_general(
        expand_matrix, local_coeff, (((1,), (1,)), ((), ())), preferred_element_type=jnp.float32
    ).astype(jnp.bfloat16)
    result = jnp.einsum(
        "icj,jb->icb", downward_matrix, local_moment, preferred_element_type=jnp.float32
    )
    return result.reshape(surface, 8 * box_count).astype(jnp.bfloat16)


def solution(mesh):
    return jax.shard_map(
        on_device,
        mesh=mesh,
        in_specs=(
            P(None, ("grp", "sub")),
            P(),
            P(),
            P(),
            P(),
            P(),
            P(None, ("grp", "sub")),
            P(("grp", "sub"), None),
        ),
        out_specs=P(None, ("grp", "sub")),
        check_vma=False,
    )
```

profile of v0, /device:TPU:0, one launch (start us, length us, event | category | flops | bytes accessed | tf_op | source)
XLA Modules:
  0.0 130.0 jit_solution(3072430982074390626)
XLA Ops:
  0.0 0.0 copy-start
  0.0 0.0 copy-start.3
  0.0 0.8 fusion.31
  0.8 1.2 copy.30
  2.0 4.3 %copy.19 = bf16[294,8,294]{0,1,2:T(8,128)(2,1)} copy(bf16[294,8,294]{2,1,0:T(8,128)(2,1)} %param.9) | data formatting | bytes 2765952 | tf_op args[1]
  6.3 0.0 copy-done.3
  6.3 0.0 copy-start.1
  6.3 2.4 %fusion.11 = bf16[128,64]{0,1:T(8,128)(2,1)S(1)} fusion(bf16[64,294]{1,0:T(8,128)(2,1)S(1)} %copy-done.3, bf16[294,8,294]{0,1,2:T(8,128)(2,1)} %copy.19, bf16[296,8,128]{2,1,0:T(8,128)(2,1)S(1)} %bitcast.79), kind=kOutput, calls=%fused_computation.11 | convolution fusion | flops 181883648 | bytes 2050624 | tf_op jit(solution)/shard_map/dot_general | solution.py:24
  8.7 0.1 copy.29
  8.8 0.7 gather_fusion
  9.5 0.7 reshape.67
  10.2 7.3 %all-to-all-start = ((bf16[8,2,320]{2,1,0:T(2,128)(2,1)}), bf16[8,2,320]{2,1,0:T(2,128)(2,1)S(1)}, u32[]{:S(2)}, u32[]{:S(2)}) async-start(bf16[8,2,320]{2,1,0:T(2,128)(2,1)} %reshape.67), calls=%async_computation | async-start | bytes 24576 | tf_op jit(solution)/shard_map/all_to_all | solution.py:31
  17.5 0.0 copy-done.1
  17.5 0.4 compare_select_fusion
  17.9 0.1 copy.24
  18.0 0.2 reshape.54
  18.2 5.8 %all-to-all-done = bf16[8,2,320]{2,1,0:T(2,128)(2,1)S(1)} async-done(((bf16[8,2,320]{2,1,0:T(2,128)(2,1)}), bf16[8,2,320]{2,1,0:T(2,128)(2,1)S(1)}, u32[]{:S(2)}, u32[]{:S(2)}) %all-to-all-start) | async-done | bytes 10272 | tf_op jit(solution)/shard_map/all_to_all | solution.py:31
  24.0 0.1 reshape.68
  24.1 0.1 copy.21
  24.2 5.4 %all-gather = bf16[4,208,64]{1,2,0:T(8,128)(2,1)S(1)} all-gather(bf16[1,208,64]{1,2,0:T(8,128)(2,1)S(1)} %maximum_bitcast_fusion), channel_id=1, replica_groups=mesh['grp'=8,'sub'=4] {'sub'}, dimensions={0}, use_global_device_ids=true | all-gather | bytes 133120 | tf_op jit(solution)/shard_map/all_gather | solution.py:44
  29.7 0.2 copy.27
  29.9 81.2 %gather_fusion.1 = bf16[40448,64]{1,0:T(8,128)(2,1)} fusion(bf16[833,64]{1,0:T(8,128)(2,1)S(1)} %concatenate.11, s32[40960]{0:T(1024)S(1)} %pad_clamp_fusion), kind=kCustom, calls=%fused_computation.1 | custom fusion | bytes 10516480 | tf_op jit(solution)/shard_map/gather | solution.py:50
  111.0 0.0 copy-start.2
  111.0 11.3 %reshape.43 = bf16[128,20224]{1,0:T(8,128)(2,1)} reshape(bf16[40448,64]{1,0:T(8,128)(2,1)} %gather_fusion.1) | data formatting | bytes 10354688 | tf_op jit(solution)/shard_map/reshape | solution.py:50
  122.3 0.0 copy-done
  122.3 0.0 copy-done.2
  122.3 4.5 %fusion.9 = bf16[128,294,1]{0,1,2:T(8,128)(2,1)S(1)} fusion(bf16[294,64]{0,1:T(8,128)(2,1)S(1)} %copy-done.2, bf16[128,20224]{1,0:T(8,128)(2,1)} %reshape.43, bf16[64,20224]{1,0:T(8,128)(2,1)S(1)} %copy-done), kind=kOutput, calls=%fused_computation.9 | convolution fusion | flops 336212736 | bytes 7878912 | tf_op jit(solution)/shard_map/dot_general | solution.py:55
  126.8 2.1 %fusion.5 = bf16[294,8,128]{2,0,1:T(8,128)(2,1)S(1)} fusion(bf16[128,294,1]{0,1,2:T(8,128)(2,1)S(1)} %fusion.9, bf16[294,8,294]{2,1,0:T(8,128)(2,1)} %param.13), kind=kOutput, calls=%fused_computation.5 | convolution fusion | flops 177321984 | bytes 2060352 | tf_op jit(solution)/shard_map/icj,jb->icb/dot_general | solution.py:58
  129.0 0.1 copy.26
  129.1 0.9 copy.31
  (8 shorter events, 0.2 us)
Async XLA Ops:
  0.0 122.3 %copy-start = (bf16[64,20224]{1,0:T(8,128)(2,1)S(1)}, bf16[64,20224]{1,0:T(8,128)(2,1)}, u32[]{:S(2)}) copy-start(bf16[64,20224]{1,0:T(8,128)(2,1)} %param.11) | copy-start | bytes 7766020
  0.0 6.3 %copy-start.3 = (bf16[64,294]{1,0:T(8,128)(2,1)S(1)}, bf16[64,294]{1,0:T(8,128)(2,1)}, u32[]{:S(2)}) copy-start(bf16[64,294]{1,0:T(8,128)(2,1)} %param.10) | copy-start | bytes 112900
  6.3 11.2 %copy-start.1 = (s32[316,128]{1,0:T(8,128)S(1)}, s32[316,128]{1,0:T(8,128)}, u32[]{:S(2)}) copy-start(s32[316,128]{1,0:T(8,128)} %param.14) | copy-start | bytes 485380
  10.2 13.8 %all-to-all-start = ((bf16[8,2,320]{2,1,0:T(2,128)(2,1)}), bf16[8,2,320]{2,1,0:T(2,128)(2,1)S(1)}, u32[]{:S(2)}, u32[]{:S(2)}) async-start(bf16[8,2,320]{2,1,0:T(2,128)(2,1)} %reshape.67), calls=%async_computation | async-start | bytes 24576 | tf_op jit(solution)/shard_map/all_to_all | solution.py:31
  111.0 11.3 %copy-start.2 = (bf16[294,64]{0,1:T(8,128)(2,1)S(1)}, bf16[294,64]{0,1:T(8,128)(2,1)}, u32[]{:S(2)}) copy-start(bf16[294,64]{0,1:T(8,128)(2,1)} %param.12) | copy-start | bytes 112900
where the time goes:
time: 131 us; the launch traced here: 130 us
  local copies, waits for them, and re-layouts  101 us (77%)
  matrix products  9.03 us (7%)
  starting transfers between devices  7.28 us (6%)
  waiting for transfers between devices  5.77 us (4%)
  blocking collectives  5.42 us (4%)
    gather x1, local copies, waits for them, and re-layouts, on_device(): picked = extended[index].reshape(box_count, -1)  81.2 us
    reshape x1, local copies, waits for them, and re-layouts, on_device(): picked = extended[index].reshape(box_count, -1)  11.3 us
    unnamed x16, local copies, waits for them, and re-layouts  7.47 us
    all_to_all x1, starting transfers between devices, on_device(): lax.all_to_all(source, 'grp', split_axis=0, concat_axis=0, tiled=True)  7.28 us
    all_to_all x1, waiting for transfers between devices, on_device(): lax.all_to_all(source, 'grp', split_axis=0, concat_axis=0, tiled=True)  5.77 us
    all_gather x1, blocking collectives, on_device(): whole_pool = lax.all_gather(mine, 'sub', axis=0, tiled=True)  5.42 us
    dot_general x1, matrix products, on_device(): lax.dot_general(expand_matrix, local_coeff, (((1,), (1,)), ((), ())), pre...  4.52 us
  transfers between devices with their start and end apart: 1, of which 1 were waited for; matrix products, arithmetic and copies ran while one was open for 1% of the time, Pallas kernels for 0%

commit v1 on v0

v1 whole, which is shorter than its diff:
```python
import functools

import jax
import jax.numpy as jnp
from jax import lax
from jax.experimental import pallas as pl
from jax.experimental.pallas import tpu as pltpu
from jax.sharding import PartitionSpec as P

LANES = 128
VMEM = pl.BlockSpec(memory_space=pltpu.VMEM)
SMEM = pl.BlockSpec(memory_space=pltpu.SMEM)


def lane_gather(values, lanes):
    numbers = lax.GatherDimensionNumbers(
        offset_dims=(),
        collapsed_slice_dims=(1,),
        start_index_map=(1,),
        operand_batching_dims=(0,),
        start_indices_batching_dims=(0,),
    )
    return lax.gather(
        values,
        lanes[..., None],
        numbers,
        slice_sizes=(1, 1),
        mode=lax.GatherScatterMode.PROMISE_IN_BOUNDS,
    )


def chunks_of(total, size):
    return [(at, min(size, total - at)) for at in range(0, total, size)]


def upward_kernel(rows_per, x_ref, u_ref, p_ref, map_ref, packed_ref, ghost_ref, wide, parent, slots):
    surface = x_ref.shape[0]
    coeff = p_ref.shape[0]
    for at, size in chunks_of(surface, 96):
        for n, (left, width) in enumerate(chunks_of(surface, LANES)):
            wide[n, pl.ds(at * 8, size * 8), 0:width] = u_ref[
                pl.ds(at * 8, size * 8), left : left + width
            ].astype(jnp.float32)
        total = jnp.zeros((size, LANES), jnp.float32)
        for c in range(8):
            matrix = jnp.concatenate(
                [
                    wide.at[n][pl.ds(at * 8 + c, size, stride=8), :].astype(jnp.bfloat16)[:, :width]
                    for n, (_, width) in enumerate(chunks_of(surface, LANES))
                ],
                axis=1,
            )
            total += jnp.dot(
                matrix,
                x_ref[:, c * LANES : (c + 1) * LANES],
                preferred_element_type=jnp.float32,
            )
        parent[pl.ds(at, size), :] = total.astype(jnp.bfloat16)
    packed = jnp.dot(p_ref[...], parent[...], preferred_element_type=jnp.float32)
    packed = packed.astype(jnp.bfloat16)
    packed_ref[...] = packed
    width = slots.shape[1]
    slots[...] = jnp.full(slots.shape, LANES, jnp.int32)
    slots[:, 0 : map_ref.shape[1]] = map_ref[...]
    for at in range(0, width, LANES):
        ids = jnp.broadcast_to(slots[:, at : at + LANES], (coeff, LANES))
        taken = lane_gather(packed, (ids & (LANES - 1)).astype(jnp.int16)).astype(jnp.float32)
        taken = jnp.where(ids < LANES, taken, 0.0)
        rows = jnp.transpose(taken).astype(jnp.bfloat16)
        keep = min(LANES, map_ref.shape[1] - at)
        ghost_ref[at : at + keep, :] = rows[:keep, :]


def pick(index_row, tile_row, tiles, pool_ref, coeff, names):
    lanes = jnp.broadcast_to(index_row, (coeff, LANES)).astype(jnp.int16)
    place = jnp.broadcast_to(tile_row, (coeff, LANES)).astype(jnp.int16)
    out = jnp.zeros((coeff, LANES), jnp.bfloat16)
    if tiles <= 8:
        for k in range(tiles):
            got = lane_gather(pool_ref[:, k * LANES : (k + 1) * LANES], lanes)
            out = jnp.where(place == names(k), got, out)
        return out

    def one(k, out):
        got = lane_gather(pool_ref[:, pl.ds(pl.multiple_of(k * LANES, LANES), LANES)], lanes)
        return jnp.where(place == names(k), got, out)

    return lax.fori_loop(0, tiles, one, out)


def translate(index, tile, matrix_ref, pool_ref, tiles, names, unroll):
    coeff = pool_ref.shape[0]
    offsets = index.shape[0]
    group = 4

    def block(at, count):
        parts = [
            pick(index[pl.ds(at + n, 1), :], tile[pl.ds(at + n, 1), :], tiles, pool_ref, coeff, names)
            for n in range(count)
        ]
        return jnp.dot(
            matrix_ref[:, pl.ds(pl.multiple_of(at * coeff, LANES) if not isinstance(at, int) else at * coeff, count * coeff)],
            jnp.concatenate(parts, axis=0),
            preferred_element_type=jnp.float32,
        )

    step = group * unroll
    trips = offsets // step

    def body(i, total):
        for n in range(unroll):
            total += block(i * step + n * group, group)
        return total

    total = lax.fori_loop(0, trips, body, jnp.zeros((coeff, LANES), jnp.float32))
    for at, count in chunks_of(offsets - trips * step, group):
        total += block(trips * step + at, count)
    return total


def own_kernel(me_ref, list_ref, matrix_ref, pool_ref, out_ref, index, tile):
    me = me_ref[0, 0]
    lists = list_ref[...]
    index[...] = lists & (LANES - 1)
    tile[...] = (lists // LANES) ^ me
    tiles = pool_ref.shape[1] // LANES
    out_ref[...] = translate(
        index, tile, matrix_ref, pool_ref, tiles, lambda k: jnp.int16(k), 4
    )


def ghost_kernel(
    own_boxes, list_ref, matrix_ref, rows_ref, own_ref, e_ref, d_ref, out_ref, index, tile, pool, wide
):
    coeff = matrix_ref.shape[0]
    surface = e_ref.shape[0]
    count = rows_ref.shape[0]
    lists = list_ref[...] - own_boxes
    index[...] = lists & (LANES - 1)
    tile[...] = jnp.where((lists >= 0) & (lists < count), lists >> 7, -1)
    for at, size in chunks_of(count, LANES):
        rows = rows_ref[at : at + size, :].astype(jnp.float32)
        if size < LANES:
            rows = jnp.concatenate([rows, jnp.zeros((LANES - size, coeff), jnp.float32)], axis=0)
        pool[:, at : at + LANES] = jnp.transpose(rows).astype(jnp.bfloat16)
    tiles = pool.shape[1] // LANES
    total = translate(index, tile, matrix_ref, pool, tiles, lambda k: jnp.int16(k), 4)
    local_coeff = (total + own_ref[...]).astype(jnp.bfloat16)
    moment = jnp.dot(e_ref[...], local_coeff, preferred_element_type=jnp.float32)
    moment = moment.astype(jnp.bfloat16)
    for at, size in chunks_of(surface, 96):
        wide[pl.ds(at * 8, size * 8), :] = jnp.dot(
            d_ref[pl.ds(at * 8, size * 8), :], moment, preferred_element_type=jnp.float32
        )
        for c in range(8):
            out_ref[pl.ds(at, size), c * LANES : (c + 1) * LANES] = wide[
                pl.ds(at * 8 + c, size, stride=8), :
            ].astype(jnp.bfloat16)


def on_device(
    child_moments,
    upward_matrix,
    project_matrix,
    transfer_matrix,
    expand_matrix,
    downward_matrix,
    neighbour_list,
    ghost_map,
):
    surface = child_moments.shape[0]
    boxes = child_moments.shape[1] // 8
    coeff = project_matrix.shape[0]
    slots = ghost_map.shape[1]
    offsets = neighbour_list.shape[0]
    grp_count = lax.axis_size("grp")
    sub_count = lax.axis_size("sub")
    if boxes != LANES or sub_count & (sub_count - 1):
        raise ValueError("unsupported sizes")
    slot_lanes = -(-slots // LANES) * LANES
    packed, ghosts = pl.pallas_call(
        functools.partial(upward_kernel, 96),
        out_shape=(
            jax.ShapeDtypeStruct((coeff, boxes), jnp.bfloat16),
            jax.ShapeDtypeStruct((slots, coeff), jnp.bfloat16),
        ),
        in_specs=[VMEM] * 4,
        out_specs=(VMEM, VMEM),
        scratch_shapes=[
            pltpu.VMEM((-(-surface // LANES), surface * 8, LANES), jnp.float32),
            pltpu.VMEM((surface, boxes), jnp.bfloat16),
            pltpu.VMEM((1, slot_lanes), jnp.int32),
        ],
        compiler_params=pltpu.CompilerParams(vmem_limit_bytes=16 << 20),
        name="upward",
    )(
        child_moments,
        upward_matrix.reshape(surface * 8, surface),
        project_matrix,
        ghost_map,
    )
    send = jnp.broadcast_to(ghosts[None], (sub_count, slots, coeff)).reshape(sub_count * slots, coeff)
    received = lax.all_to_all(send, ("sub", "grp"), split_axis=0, concat_axis=0, tiled=True)
    own = packed
    hop = 1
    while hop < sub_count:
        other = lax.ppermute(own, "sub", [(i, i ^ hop) for i in range(sub_count)])
        own = jnp.concatenate([own, other], axis=1)
        hop *= 2
    me = lax.axis_index("sub").astype(jnp.int32).reshape(1, 1)
    own_part = pl.pallas_call(
        own_kernel,
        out_shape=jax.ShapeDtypeStruct((coeff, boxes), jnp.float32),
        in_specs=[SMEM] + [VMEM] * 3,
        out_specs=VMEM,
        scratch_shapes=[pltpu.VMEM((offsets, boxes), jnp.int32)] * 2,
        compiler_params=pltpu.CompilerParams(vmem_limit_bytes=16 << 20),
        cost_estimate=pl.CostEstimate(flops=2_000_000_000, bytes_accessed=1, transcendentals=0),
        name="own",
    )(me, neighbour_list, transfer_matrix, own)
    ghost_count = received.shape[0]
    ghost_lanes = -(-ghost_count // LANES) * LANES
    result = pl.pallas_call(
        functools.partial(ghost_kernel, sub_count * boxes),
        out_shape=jax.ShapeDtypeStruct((surface, 8 * boxes), jnp.bfloat16),
        in_specs=[VMEM] * 6,
        out_specs=VMEM,
        scratch_shapes=[pltpu.VMEM((offsets, boxes), jnp.int32)] * 2
        + [
            pltpu.VMEM((coeff, ghost_lanes), jnp.bfloat16),
            pltpu.VMEM((surface * 8, boxes), jnp.float32),
        ],
        compiler_params=pltpu.CompilerParams(vmem_limit_bytes=24 << 20),
        name="ghost_downward",
    )(
        neighbour_list,
        transfer_matrix,
        received,
        own_part,
        expand_matrix,
        downward_matrix.reshape(surface * 8, surface),
    )
    return result


def solution(mesh):
    return jax.shard_map(
        on_device,
        mesh=mesh,
        in_specs=(
            P(None, ("grp", "sub")),
            P(),
            P(),
            P(),
            P(),
            P(),
            P(None, ("grp", "sub")),
            P(("grp", "sub"), None),
        ),
        out_specs=P(None, ("grp", "sub")),
        check_vma=False,
    )
```

time: 131 us -> 43 us (0.33)
  local copies, waits for them, and re-layouts: 101 us -> 6.73 us
  Pallas kernels: 0 us -> 26.8 us
  matrix products: 9.03 us -> 0 us
  blocking collectives: 5.42 us -> 0 us
  waiting for transfers between devices: 5.77 us -> 0.84 us
    gather x2 -> x0, local copies, waits for them, and re-layouts: 81.8 us -> none  [the longest x1 81.2 us: on_device(): picked = extended[index].reshape(box_count, -1)]
    pallas_call x0 -> x3, Pallas kernels: none -> 26.8 us  [the longest x1 13 us: on_device(): pl.pallas_call(functools.partial(ghost_kernel, sub_count * boxes), out_sh...]
    reshape x1 -> x0, local copies, waits for them, and re-layouts: 11.3 us -> none  [on_device(): picked = extended[index].reshape(box_count, -1)]
    dot_general x3 -> x0, matrix products: 9.03 us -> none  [the longest x1 4.52 us: on_device(): lax.dot_general(expand_matrix, local_coeff, (((1,), (1,)), ((), ())), pre...]
    all_to_all x1, waiting for transfers between devices: 5.77 us -> 0.01 us  [on_device(): lax.all_to_all(send, ('sub', 'grp'), split_axis=0, concat_axis=0, tiled=T...]
    all_gather x1 -> x0, blocking collectives: 5.42 us -> none  [on_device(): whole_pool = lax.all_gather(mine, 'sub', axis=0, tiled=True)]
    ppermute x0 -> x2, starting transfers between devices: none -> 3.4 us  [on_device(): other = lax.ppermute(own, 'sub', [(i, i ^ hop) for i in range(sub_count)])]
    all_to_all x1, starting transfers between devices: 7.28 us -> 4.89 us  [on_device(): lax.all_to_all(send, ('sub', 'grp'), split_axis=0, concat_axis=0, tiled=T...]
  transfers between devices with their start and end apart: 1 -> 3, of which waited for: 1 -> 1; matrix products, arithmetic and copies ran while one was open for 1% -> 2% of each run, Pallas kernels for 0% -> 29%
where the time goes in v1:
time: 43 us; the launch traced here: 42.8 us
  Pallas kernels  26.8 us (62%)
  starting transfers between devices  8.29 us (19%)
  local copies, waits for them, and re-layouts  6.73 us (16%)
  waiting for transfers between devices  0.84 us (2%)
    pallas_call x1, Pallas kernels, on_device(): pl.pallas_call(functools.partial(ghost_kernel, sub_count * boxes), out_sh...  13 us
    pallas_call x1, Pallas kernels, on_device(): pl.pallas_call(own_kernel, out_shape=jax.ShapeDtypeStruct((coeff, boxes),...  12.3 us
    unnamed x19, local copies, waits for them, and re-layouts  6.64 us
    all_to_all x1, starting transfers between devices, on_device(): lax.all_to_all(send, ('sub', 'grp'), split_axis=0, concat_axis=0, tiled=T...  4.89 us
    ppermute x2, starting transfers between devices, on_device(): other = lax.ppermute(own, 'sub', [(i, i ^ hop) for i in range(sub_count)])  3.4 us
    pallas_call x1, Pallas kernels, on_device(): pl.pallas_call(functools.partial(upward_kernel, 96), out_shape=(jax.Shape...  1.52 us
  transfers between devices with their start and end apart: 3, of which 1 were waited for; matrix products, arithmetic and copies ran while one was open for 2% of the time, Pallas kernels for 29%

profile of v1, /device:TPU:0, one launch (start us, length us, event | category | flops | bytes accessed | tf_op | source)
XLA Modules:
  0.0 42.8 jit_solution(14547040041976748929)
XLA Ops:
  0.0 0.0 copy-start
  0.0 0.0 copy-start.1
  0.0 1.6 %copy-done.1 = bf16[294,8,294]{2,1,0:T(8,128)(2,1)S(1)} copy-done((bf16[294,8,294]{2,1,0:T(8,128)(2,1)S(1)}, bf16[294,8,294]{2,1,0:T(8,128)(2,1)}, u32[]{:S(2)}) %copy-start.1) | copy-done | bytes 1383000
  1.6 0.0 copy-start.3
  1.6 1.1 %copy-done.3 = bf16[294,1024]{1,0:T(8,128)(2,1)S(1)} copy-done((bf16[294,1024]{1,0:T(8,128)(2,1)S(1)}, bf16[294,1024]{1,0:T(8,128)(2,1)}, u32[]{:S(2)}) %copy-start.3) | copy-done | bytes 602136
  2.7 0.0 copy-start.5
  2.7 0.8 %copy-done.5 = bf16[64,294]{1,0:T(8,128)(2,1)S(1)} copy-done((bf16[64,294]{1,0:T(8,128)(2,1)S(1)}, bf16[64,294]{1,0:T(8,128)(2,1)}, u32[]{:S(2)}) %copy-start.5) | copy-done | bytes 37656
  3.5 0.0 copy-start.6
  3.5 0.7 %copy-done.6 = s32[1,80]{1,0:T(1,128)S(1)} copy-done((s32[1,80]{1,0:T(1,128)S(1)}, s32[1,80]{1,0:T(1,128)}, u32[]{:S(2)}) %copy-start.6) | copy-done | bytes 344
  4.2 0.0 copy-start.7
  4.2 0.0 copy-start.4
  4.2 1.5 %upward.1 = (bf16[64,128]{1,0:T(8,128)(2,1)S(1)}, bf16[80,64]{1,0:T(8,128)(2,1)S(1)}) custom-call(bf16[294,1024]{1,0:T(8,128)(2,1)S(1)} %copy-done.3, bf16[2352,294]{1,0:T(8,128)(2,1)S(1)} %bitcast.3, bf16[64,294]{1,0:T(8,128)(2,1)S(1)} %copy-done.5, s32[1,80]{1,0:T(1,128)S(1)} %copy-done.6), custom_call_target="tpu_custom_call" | custom-call | tf_op jit(solution)/shard_map/upward/pallas_call | solution.py:181
  5.7 0.6 %collective-permute-start = (bf16[64,128]{1,0:T(8,128)(2,1)S(1)}, bf16[64,128]{1,0:T(8,128)(2,1)S(1)}, u32[]{:S(2)}, u32[]{:S(2)}) collective-permute-start(bf16[64,128]{1,0:T(8,128)(2,1)S(1)} %get-tuple-element.8), channel_id=1, source_target_pairs={{0,1},{1,0},{2,3},{3,2},{4,5},{5,4},{6,7},{7,6},{8,9},{9,8},{10,11... | collective-permute-start | bytes 49160 | tf_op jit(solution)/shard_map/ppermute | solution.py:207
  6.3 0.8 %collective-permute-done = bf16[64,128]{1,0:T(8,128)(2,1)S(1)} collective-permute-done((bf16[64,128]{1,0:T(8,128)(2,1)S(1)}, bf16[64,128]{1,0:T(8,128)(2,1)S(1)}, u32[]{:S(2)}, u32[]{:S(2)}) %collective-permute-start) | collective-permute-done | bytes 16416 | tf_op jit(solution)/shard_map/ppermute | solution.py:207
  7.1 2.8 %collective-permute-start.1 = (bf16[64,256]{1,0:T(8,128)(2,1)S(1)}, bf16[64,256]{1,0:T(8,128)(2,1)S(1)}, u32[]{:S(2)}, u32[]{:S(2)}) collective-permute-start(bf16[64,256]{1,0:T(8,128)(2,1)S(1)} %pad_maximum_fusion.1), channel_id=1, source_target_pairs={{0,2},{1,3},{2,0},{3,1},{4,6},{5,7},{6,4},{7,5},{8,10},{9,11},{10,... | collective-permute-start | bytes 98312 | tf_op jit(solution)/shard_map/ppermute | solution.py:207
  10.0 0.7 %reshape.17 = bf16[32,2,320]{2,1,0:T(2,128)(2,1)} reshape(bf16[32,10,64]{2,1,0:T(8,128)(2,1)S(1)} %all_to_all.7) | data formatting | bytes 81920
  10.7 4.9 %all-to-all-start = ((bf16[32,2,320]{2,1,0:T(2,128)(2,1)}), bf16[32,2,320]{2,1,0:T(2,128)(2,1)S(1)}, u32[]{:S(2)}, u32[]{:S(2)}) async-start(bf16[32,2,320]{2,1,0:T(2,128)(2,1)} %reshape.17), calls=%async_computation | async-start | bytes 98304 | tf_op jit(solution)/shard_map/all_to_all | solution.py:203
  15.6 0.0 copy-done.7
  15.7 0.1 copy.10.e_ref
  15.8 0.0 collective-permute-done.1
  15.8 0.0 copy-done
  15.8 0.0 copy-done.4
  15.8 12.3 %own.1.own_ref = f32[64,128]{1,0:T(8,128)S(1)} custom-call(s32[1,1]{1,0:T(1,128)} %bitcast.1.me_ref, s32[316,128]{1,0:T(8,128)S(1)} %copy-done.4, bf16[64,20224]{1,0:T(8,128)(2,1)S(1)} %copy-done, bf16[64,512]{1,0:T(8,128)(2,1)S(1)} %pad_maximum_fusion.pool_ref), custom_call_target="tpu_custom_call" | custom-call | flops 2000000000 | bytes 1 | tf_op jit(solution)/shard_map/own/pallas_call | solution.py:211
  28.1 0.0 all-to-all-done
  28.1 0.1 reshape.18
  28.3 0.0 copy-start.2
  28.3 1.5 %copy-done.2 = bf16[294,8,294]{2,1,0:T(8,128)(2,1)S(1)} copy-done((bf16[294,8,294]{2,1,0:T(8,128)(2,1)S(1)}, bf16[294,8,294]{2,1,0:T(8,128)(2,1)}, u32[]{:S(2)}) %copy-start.2) | copy-done | bytes 1383000
  29.8 13.0 %ghost_downward.1 = bf16[294,1024]{1,0:T(8,128)(2,1)} custom-call(s32[316,128]{1,0:T(8,128)S(1)} %copy-done.4, bf16[64,20224]{1,0:T(8,128)(2,1)S(1)} %copy-done, bf16[320,64]{1,0:T(8,128)(2,1)S(1)} %all_to_all.9.rows_ref, f32[64,128]{1,0:T(8,128)S(1)} %own.1.own_ref, bf16[294,64]{1,0:T(8,128)(2,1)S(1)} %copy.10.e_ref, bf16[2352,294]{1,0:T(8,128)(2,1)S(1)} %bitcast.4), custom_call_target="tpu_custom_call" | custom-call | tf_op jit(solution)/shard_map/ghost_downward/pallas_call | solution.py:223
  (5 shorter events, 0.1 us)
Async XLA Ops:
  0.0 15.8 %copy-start = (bf16[64,20224]{1,0:T(8,128)(2,1)S(1)}, bf16[64,20224]{1,0:T(8,128)(2,1)}, u32[]{:S(2)}) copy-start(bf16[64,20224]{1,0:T(8,128)(2,1)} %matrix_ref.3) | copy-start | bytes 7766020
  0.0 1.6 %copy-start.1 = (bf16[294,8,294]{2,1,0:T(8,128)(2,1)S(1)}, bf16[294,8,294]{2,1,0:T(8,128)(2,1)}, u32[]{:S(2)}) copy-start(bf16[294,8,294]{2,1,0:T(8,128)(2,1)} %param.9) | copy-start | bytes 4148932
  1.6 1.1 %copy-start.3 = (bf16[294,1024]{1,0:T(8,128)(2,1)S(1)}, bf16[294,1024]{1,0:T(8,128)(2,1)}, u32[]{:S(2)}) copy-start(bf16[294,1024]{1,0:T(8,128)(2,1)} %x_ref.1) | copy-start | bytes 1806340
  2.7 0.8 %copy-start.5 = (bf16[64,294]{1,0:T(8,128)(2,1)S(1)}, bf16[64,294]{1,0:T(8,128)(2,1)}, u32[]{:S(2)}) copy-start(bf16[64,294]{1,0:T(8,128)(2,1)} %p_ref.1) | copy-start | bytes 112900
  3.5 0.7 %copy-start.6 = (s32[1,80]{1,0:T(1,128)S(1)}, s32[1,80]{1,0:T(1,128)}, u32[]{:S(2)}) copy-start(s32[1,80]{1,0:T(1,128)} %map_ref.1) | copy-start | bytes 964
  4.2 11.5 %copy-start.7 = (bf16[294,64]{0,1:T(8,128)(2,1)S(1)}, bf16[294,64]{0,1:T(8,128)(2,1)}, u32[]{:S(2)}) copy-start(bf16[294,64]{0,1:T(8,128)(2,1)} %param.12) | copy-start | bytes 112900
  4.2 11.6 %copy-start.4 = (s32[316,128]{1,0:T(8,128)S(1)}, s32[316,128]{1,0:T(8,128)}, u32[]{:S(2)}) copy-start(s32[316,128]{1,0:T(8,128)} %list_ref.3) | copy-start | bytes 485380
  5.7 1.4 %collective-permute-start = (bf16[64,128]{1,0:T(8,128)(2,1)S(1)}, bf16[64,128]{1,0:T(8,128)(2,1)S(1)}, u32[]{:S(2)}, u32[]{:S(2)}) collective-permute-start(bf16[64,128]{1,0:T(8,128)(2,1)S(1)} %get-tuple-element.8), channel_id=1, source_target_pairs={{0,1},{1,0},{2,3},{3,2},{4,5},{5,4},{6,7},{7,6},{8,9},{9,8},{10,11... | collective-permute-start | bytes 49160 | tf_op jit(solution)/shard_map/ppermute | solution.py:207
  7.1 8.7 %collective-permute-start.1 = (bf16[64,256]{1,0:T(8,128)(2,1)S(1)}, bf16[64,256]{1,0:T(8,128)(2,1)S(1)}, u32[]{:S(2)}, u32[]{:S(2)}) collective-permute-start(bf16[64,256]{1,0:T(8,128)(2,1)S(1)} %pad_maximum_fusion.1), channel_id=1, source_target_pairs={{0,2},{1,3},{2,0},{3,1},{4,6},{5,7},{6,4},{7,5},{8,10},{9,11},{10,... | collective-permute-start | bytes 98312 | tf_op jit(solution)/shard_map/ppermute | solution.py:207
  10.7 17.4 %all-to-all-start = ((bf16[32,2,320]{2,1,0:T(2,128)(2,1)}), bf16[32,2,320]{2,1,0:T(2,128)(2,1)S(1)}, u32[]{:S(2)}, u32[]{:S(2)}) async-start(bf16[32,2,320]{2,1,0:T(2,128)(2,1)} %reshape.17), calls=%async_computation | async-start | bytes 98304 | tf_op jit(solution)/shard_map/all_to_all | solution.py:203
  28.3 1.5 %copy-start.2 = (bf16[294,8,294]{2,1,0:T(8,128)(2,1)S(1)}, bf16[294,8,294]{2,1,0:T(8,128)(2,1)}, u32[]{:S(2)}) copy-start(bf16[294,8,294]{2,1,0:T(8,128)(2,1)} %param.13) | copy-start | bytes 4148932

commit v2 on v1

v2 whole, which is shorter than its diff:
```python
import functools

import jax
import jax.numpy as jnp
from jax import lax
from jax.experimental import pallas as pl
from jax.experimental.pallas import tpu as pltpu
from jax.sharding import PartitionSpec as P

LANES = 128
VMEM = pl.BlockSpec(memory_space=pltpu.VMEM)
HBM = pl.BlockSpec(memory_space=pltpu.HBM)
SMEM = pl.BlockSpec(memory_space=pltpu.SMEM)


def lane_gather(values, lanes):
    numbers = lax.GatherDimensionNumbers(
        offset_dims=(),
        collapsed_slice_dims=(1,),
        start_index_map=(1,),
        operand_batching_dims=(0,),
        start_indices_batching_dims=(0,),
    )
    return lax.gather(
        values,
        lanes[..., None],
        numbers,
        slice_sizes=(1, 1),
        mode=lax.GatherScatterMode.PROMISE_IN_BOUNDS,
    )


def chunks_of(total, size):
    return [(at, min(size, total - at)) for at in range(0, total, size)]


def upward_kernel(x_hbm, u_hbm, p_hbm, map_hbm, packed_ref, ghost_ref, x_ref, u_ref, p_ref, map_ref, slots, wide, parent, sems):
    surface = x_ref.shape[0]
    coeff = p_ref.shape[0]
    used = map_hbm.shape[1]
    chunks = chunks_of(surface, 96)
    x_copy = pltpu.make_async_copy(x_hbm, x_ref, sems.at[0])
    x_copy.start()
    u_copies = []
    for n, (at, size) in enumerate(chunks):
        rows = pl.ds(at * 8, size * 8)
        u_copies.append(pltpu.make_async_copy(u_hbm.at[rows, :], u_ref.at[rows, :], sems.at[3 + n]))
        u_copies[-1].start()
    p_copy = pltpu.make_async_copy(p_hbm, p_ref, sems.at[1])
    p_copy.start()
    slots[...] = jnp.full(slots.shape, LANES, jnp.int32)
    map_copy = pltpu.make_async_copy(map_hbm, map_ref, sems.at[2])
    map_copy.start()
    x_copy.wait()
    for n, (at, size) in enumerate(chunks):
        u_copies[n].wait()
        for m, (left, width) in enumerate(chunks_of(surface, LANES)):
            wide[m, pl.ds(at * 8, size * 8), 0:width] = u_ref[
                pl.ds(at * 8, size * 8), left : left + width
            ].astype(jnp.float32)
        total = jnp.zeros((size, LANES), jnp.float32)
        for c in range(8):
            matrix = jnp.concatenate(
                [
                    wide.at[m][pl.ds(at * 8 + c, size, stride=8), :].astype(jnp.bfloat16)[:, :width]
                    for m, (_, width) in enumerate(chunks_of(surface, LANES))
                ],
                axis=1,
            )
            total += jnp.dot(
                matrix,
                x_ref[:, c * LANES : (c + 1) * LANES],
                preferred_element_type=jnp.float32,
            )
        parent[pl.ds(at, size), :] = total.astype(jnp.bfloat16)
    p_copy.wait()
    map_copy.wait()
    slots[:, 0:used] = map_ref[...]
    packed = jnp.dot(p_ref[...], parent[...], preferred_element_type=jnp.float32)
    packed = packed.astype(jnp.bfloat16)
    packed_ref[...] = packed
    for at in range(0, slots.shape[1], LANES):
        ids = jnp.broadcast_to(slots[:, at : at + LANES], (coeff, LANES))
        taken = lane_gather(packed, (ids & (LANES - 1)).astype(jnp.int16)).astype(jnp.float32)
        taken = jnp.where(ids < LANES, taken, 0.0)
        rows = jnp.transpose(taken).astype(jnp.bfloat16)
        keep = min(LANES, used - at)
        ghost_ref[at : at + keep, :] = rows[:keep, :]


def spread(row, rows):
    return jnp.broadcast_to(row, (rows, LANES))


def pick_lanes(code, pool_ref, coeff):
    tiles = pool_ref.shape[1] // LANES
    lanes = spread(code & (LANES - 1), coeff).astype(jnp.int16)
    place = spread(code >> 7, coeff).astype(jnp.int16)
    out = jnp.zeros((coeff, LANES), jnp.bfloat16)
    if tiles <= 8:
        for k in range(tiles):
            got = lane_gather(pool_ref[:, k * LANES : (k + 1) * LANES], lanes)
            out = jnp.where(place == jnp.int16(k), got, out)
        return out

    def one(k, out):
        got = lane_gather(pool_ref[:, pl.ds(pl.multiple_of(k * LANES, LANES), LANES)], lanes)
        return jnp.where(place == k.astype(jnp.int16), got, out)

    return lax.fori_loop(0, tiles, one, out)


def pick_pair(codes, stack_ref, coeff, count):
    runs = stack_ref.shape[0] // coeff
    wide = 2 * LANES
    marks = []
    for code in codes:
        low = spread(jnp.where(code < 0, -1, code & (wide - 1)), wide).astype(jnp.int16)
        marks.append(
            jnp.where(count == low, jnp.bfloat16(1), jnp.bfloat16(0))
        )
    got = jnp.dot(
        stack_ref[...], jnp.concatenate(marks, axis=1), preferred_element_type=jnp.float32
    )
    out = []
    for n, code in enumerate(codes):
        run = spread(code >> 8, coeff)
        best = got[0:coeff, n * LANES : (n + 1) * LANES]
        for k in range(1, runs):
            best = jnp.where(run == k, got[k * coeff : (k + 1) * coeff, n * LANES : (n + 1) * LANES], best)
        out.append(best.astype(jnp.bfloat16))
    return out


GROUP = 80
BY_DOT = 46


def translate(code_ref, matrix_ref, pool_ref, stack_ref, picked):
    coeff = pool_ref.shape[0]
    offsets = code_ref.shape[0]
    small = pool_ref.shape[1] // LANES <= 8
    if small:
        for k in range(stack_ref.shape[0] // coeff):
            left = k * 2 * LANES
            part = pool_ref[:, left : min(left + 2 * LANES, pool_ref.shape[1])]
            if part.shape[1] < 2 * LANES:
                part = jnp.concatenate([part, jnp.zeros((coeff, LANES), jnp.bfloat16)], axis=1)
            stack_ref[k * coeff : (k + 1) * coeff, :] = part
    count_in_run = lax.broadcasted_iota(jnp.int32, (2 * LANES, LANES), 0).astype(jnp.int16)

    def picks(at, count):
        by_dot = min(BY_DOT, count) // 2 * 2 if small else 0
        done = 0
        for n in range(count - by_dot + by_dot // 2):
            total = count - by_dot + by_dot // 2
            pairs = by_dot // 2
            if (n + 1) * pairs // total > n * pairs // total:
                rows = [code_ref[pl.ds(at + done + m, 1), :] for m in (0, 1)]
                keep(at + done, pick_pair(rows, stack_ref, coeff, count_in_run))
                done += 2
            else:
                keep(at + done, [pick_lanes(code_ref[pl.ds(at + done, 1), :], pool_ref, coeff)])
                done += 1

    def keep(at, parts):
        for n, part in enumerate(parts):
            picked[pl.ds(pl.multiple_of((at + n) * coeff, coeff), coeff), :] = part

    def product(at, count):
        start = pl.multiple_of(at * coeff, LANES)
        return jnp.dot(
            matrix_ref[:, pl.ds(start, count * coeff)],
            picked[pl.ds(start, count * coeff), :],
            preferred_element_type=jnp.float32,
        )

    trips = offsets // GROUP
    rest = offsets - trips * GROUP
    picks(0, GROUP)

    def body(i, total):
        total += product((i - 1) * GROUP, GROUP)
        picks(i * GROUP, GROUP)
        return total

    total = lax.fori_loop(1, trips, body, jnp.zeros((coeff, LANES), jnp.float32))
    total += product((trips - 1) * GROUP, GROUP)
    if rest:
        picks(trips * GROUP, rest)
        total += product(trips * GROUP, rest)
    return total


def translate_scratch(offsets, coeff, lanes):
    return [
        pltpu.VMEM((offsets, LANES), jnp.int32),
        pltpu.VMEM((-(-lanes // (2 * LANES)) * coeff, 2 * LANES), jnp.bfloat16),
        pltpu.VMEM((offsets * coeff, LANES), jnp.bfloat16),
    ]


def own_kernel(me_ref, list_ref, matrix_ref, pool_ref, out_ref, code, stack, picked):
    me = me_ref[0, 0]
    lists = list_ref[...]
    code[...] = jnp.where(lists < pool_ref.shape[1], lists ^ (me * LANES), -1)
    out_ref[...] = translate(code, matrix_ref, pool_ref, stack, picked)


def fold_kernel(e_ref, d_ref, down_ref):
    down_ref[...] = lax.dot_general(
        d_ref[...], e_ref[...], (((1,), (1,)), ((), ())), preferred_element_type=jnp.float32
    ).astype(jnp.bfloat16)


def ghost_kernel(own_boxes, list_ref, matrix_ref, rows_ref, own_ref, down_ref, out_ref, code, stack, picked, pool, wide):
    coeff = matrix_ref.shape[0]
    surface = out_ref.shape[0]
    slots = rows_ref.shape[0]
    lists = list_ref[...] - own_boxes
    code[...] = jnp.where(lists < slots, lists, -1)
    for at, size in chunks_of(slots, LANES):
        rows = rows_ref[at : at + size, :].astype(jnp.float32)
        if size < LANES:
            rows = jnp.concatenate([rows, jnp.zeros((LANES - size, coeff), jnp.float32)], axis=0)
        pool[:, at : at + LANES] = jnp.transpose(rows).astype(jnp.bfloat16)
    total = translate(code, matrix_ref, pool, stack, picked)
    local_coeff = (total + own_ref[...]).astype(jnp.bfloat16)
    for at, size in chunks_of(surface, 96):
        wide[pl.ds(at * 8, size * 8), :] = jnp.dot(
            down_ref[pl.ds(at * 8, size * 8), :], local_coeff, preferred_element_type=jnp.float32
        )
        for c in range(8):
            out_ref[pl.ds(at, size), c * LANES : (c + 1) * LANES] = wide[
                pl.ds(at * 8 + c, size, stride=8), :
            ].astype(jnp.bfloat16)


def on_device(
    child_moments,
    upward_matrix,
    project_matrix,
    transfer_matrix,
    expand_matrix,
    downward_matrix,
    neighbour_list,
    ghost_map,
):
    surface = child_moments.shape[0]
    boxes = child_moments.shape[1] // 8
    coeff = project_matrix.shape[0]
    slots = ghost_map.shape[1]
    offsets = neighbour_list.shape[0]
    grp_count = lax.axis_size("grp")
    sub_count = lax.axis_size("sub")
    if boxes != LANES or sub_count & (sub_count - 1):
        raise ValueError("unsupported sizes")
    slot_lanes = -(-slots // LANES) * LANES
    lane_tiles = -(-surface // LANES)
    packed, ghosts = pl.pallas_call(
        upward_kernel,
        out_shape=(
            jax.ShapeDtypeStruct((coeff, boxes), jnp.bfloat16),
            jax.ShapeDtypeStruct((slots, coeff), jnp.bfloat16),
        ),
        in_specs=[HBM] * 4,
        out_specs=(VMEM, VMEM),
        scratch_shapes=[
            pltpu.VMEM(child_moments.shape, jnp.bfloat16),
            pltpu.VMEM((surface * 8, surface), jnp.bfloat16),
            pltpu.VMEM(project_matrix.shape, jnp.bfloat16),
            pltpu.VMEM(ghost_map.shape, jnp.int32),
            pltpu.VMEM((1, slot_lanes), jnp.int32),
            pltpu.VMEM((lane_tiles, surface * 8, LANES), jnp.float32),
            pltpu.VMEM((surface, boxes), jnp.bfloat16),
            pltpu.SemaphoreType.DMA((3 + len(chunks_of(surface, 96)),)),
        ],
        compiler_params=pltpu.CompilerParams(vmem_limit_bytes=40000 << 10),
        cost_estimate=pl.CostEstimate(flops=500_000_000, bytes_accessed=3_000_000, transcendentals=0),
        name="upward",
    )(
        *(
            pltpu.with_memory_space_constraint(a, pltpu.HBM)
            for a in (child_moments, upward_matrix.reshape(surface * 8, surface), project_matrix, ghost_map)
        )
    )
    send = jnp.broadcast_to(ghosts[None], (sub_count, slots, coeff)).reshape(sub_count * slots, coeff)
    received = lax.all_to_all(send, ("sub", "grp"), split_axis=0, concat_axis=0, tiled=True)
    own = packed
    hop = 1
    while hop < sub_count:
        other = lax.ppermute(own, "sub", [(i, i ^ hop) for i in range(sub_count)])
        own = jnp.concatenate([own, other], axis=1)
        hop *= 2
    me = lax.axis_index("sub").astype(jnp.int32).reshape(1, 1)
    own_part = pl.pallas_call(
        own_kernel,
        out_shape=jax.ShapeDtypeStruct((coeff, boxes), jnp.float32),
        in_specs=[SMEM] + [VMEM] * 3,
        out_specs=VMEM,
        scratch_shapes=translate_scratch(offsets, coeff, own.shape[1]),
        compiler_params=pltpu.CompilerParams(vmem_limit_bytes=20 << 20),
        cost_estimate=pl.CostEstimate(flops=3_000_000_000, bytes_accessed=1, transcendentals=0),
        name="own",
    )(me, neighbour_list, transfer_matrix, own)
    down = pl.pallas_call(
        fold_kernel,
        out_shape=jax.ShapeDtypeStruct((surface * 8, coeff), jnp.bfloat16),
        in_specs=[VMEM] * 2,
        out_specs=VMEM,
        compiler_params=pltpu.CompilerParams(vmem_limit_bytes=8 << 20),
        cost_estimate=pl.CostEstimate(flops=500_000_000, bytes_accessed=1, transcendentals=0),
        name="fold",
    )(jnp.transpose(expand_matrix), downward_matrix.reshape(surface * 8, surface))
    ghost_count = received.shape[0]
    ghost_lanes = -(-ghost_count // LANES) * LANES
    result = pl.pallas_call(
        functools.partial(ghost_kernel, sub_count * boxes),
        out_shape=jax.ShapeDtypeStruct((surface, 8 * boxes), jnp.bfloat16),
        in_specs=[VMEM] * 5,
        out_specs=VMEM,
        scratch_shapes=translate_scratch(offsets, coeff, ghost_lanes)
        + [
            pltpu.VMEM((coeff, ghost_lanes), jnp.bfloat16),
            pltpu.VMEM((surface * 8, boxes), jnp.float32),
        ],
        compiler_params=pltpu.CompilerParams(vmem_limit_bytes=20 << 20),
        name="ghost_downward",
    )(neighbour_list, transfer_matrix, received, own_part, down)
    return result


def solution(mesh):
    return jax.shard_map(
        on_device,
        mesh=mesh,
        in_specs=(
            P(None, ("grp", "sub")),
            P(),
            P(),
            P(),
            P(),
            P(),
            P(None, ("grp", "sub")),
            P(("grp", "sub"), None),
        ),
        out_specs=P(None, ("grp", "sub")),
        check_vma=False,
    )
```

time: 43 us -> 26.2 us (0.61)
  Pallas kernels: 26.8 us -> 12.5 us
  local copies, waits for them, and re-layouts: 6.73 us -> 4.02 us
  starting transfers between devices: 8.29 us -> 9.34 us
  waiting for transfers between devices: 0.84 us -> 0.01 us
    pallas_call x1, Pallas kernels: 12.3 us -> 3.65 us  [on_device(): pl.pallas_call(own_kernel, out_shape=jax.ShapeDtypeStruct((coeff, boxes),...]
    pallas_call x1, Pallas kernels: 13 us -> 4.87 us  [on_device(): pl.pallas_call(functools.partial(ghost_kernel, sub_count * boxes), out_sh...]
    unnamed x19 -> x10, local copies, waits for them, and re-layouts: 6.64 us -> 3.02 us
    pallas_call x1 -> x2, Pallas kernels: 1.52 us -> 3.99 us  [the longest x1 3.21 us: on_device(): pl.pallas_call(upward_kernel, out_shape=(jax.ShapeDtypeStruct((coeff, box...]
    all_to_all x1, starting transfers between devices: 4.89 us -> 6.95 us  [on_device(): lax.all_to_all(send, ('sub', 'grp'), split_axis=0, concat_axis=0, tiled=T...]
    ppermute x2, starting transfers between devices: 3.4 us -> 2.39 us  [on_device(): other = lax.ppermute(own, 'sub', [(i, i ^ hop) for i in range(sub_count)])]
    all_to_all x2, local copies, waits for them, and re-layouts: 0.08 us -> 0.98 us  [on_device(): lax.all_to_all(send, ('sub', 'grp'), split_axis=0, concat_axis=0, tiled=T...]
    ppermute x2, waiting for transfers between devices: 0.84 us -> 0.01 us  [on_device(): other = lax.ppermute(own, 'sub', [(i, i ^ hop) for i in range(sub_count)])]
  transfers between devices with their start and end apart: 3 -> 3, of which waited for: 1 -> 0; matrix products, arithmetic and copies ran while one was open for 2% -> 3% of each run, Pallas kernels for 29% -> 17%
where the time goes in v2:
time: 26.2 us; the launch traced here: 26 us
  Pallas kernels  12.5 us (48%)
  starting transfers between devices  9.34 us (36%)
  local copies, waits for them, and re-layouts  4.02 us (15%)
    all_to_all x1, starting transfers between devices, on_device(): lax.all_to_all(send, ('sub', 'grp'), split_axis=0, concat_axis=0, tiled=T...  6.95 us
    pallas_call x1, Pallas kernels, on_device(): pl.pallas_call(functools.partial(ghost_kernel, sub_count * boxes), out_sh...  4.87 us
    pallas_call x1, Pallas kernels, on_device(): pl.pallas_call(own_kernel, out_shape=jax.ShapeDtypeStruct((coeff, boxes),...  3.65 us
    pallas_call x1, Pallas kernels, on_device(): pl.pallas_call(upward_kernel, out_shape=(jax.ShapeDtypeStruct((coeff, box...  3.21 us
    unnamed x10, local copies, waits for them, and re-layouts  3.02 us
    ppermute x2, starting transfers between devices, on_device(): other = lax.ppermute(own, 'sub', [(i, i ^ hop) for i in range(sub_count)])  2.39 us
    all_to_all x2, local copies, waits for them, and re-layouts, on_device(): lax.all_to_all(send, ('sub', 'grp'), split_axis=0, concat_axis=0, tiled=T...  0.98 us
    pallas_call x1, Pallas kernels, on_device(): pl.pallas_call(fold_kernel, out_shape=jax.ShapeDtypeStruct((surface * 8,...  0.77 us
  transfers between devices with their start and end apart: 3, of which 0 were waited for; matrix products, arithmetic and copies ran while one was open for 3% of the time, Pallas kernels for 17%

profile of v2, /device:TPU:0, one launch (start us, length us, event | category | flops | bytes accessed | tf_op | source)
XLA Modules:
  0.0 26.0 jit_solution(15737304744610892171)
XLA Ops:
  0.0 0.0 copy-start.3
  0.0 0.0 copy-start.2
  0.0 3.2 %upward.1 = (bf16[64,128]{1,0:T(8,128)(2,1)S(1)}, bf16[80,64]{1,0:T(8,128)(2,1)S(1)}) custom-call(bf16[294,1024]{1,0:T(8,128)(2,1)} %x_hbm.1, bf16[2352,294]{1,0:T(8,128)(2,1)} %bitcast.6, bf16[64,294]{1,0:T(8,128)(2,1)} %p_hbm.1, s32[1,80]{1,0:T(1,128)} %map_hbm.1), custom_call_target="tpu_custom_call" | custom-call | flops 500000000 | bytes 3000000 | tf_op jit(solution)/shard_map/upward/pallas_call | solution.py:260
  3.2 0.0 copy-start
  3.2 0.6 %collective-permute-start = (bf16[64,128]{1,0:T(8,128)(2,1)S(1)}, bf16[64,128]{1,0:T(8,128)(2,1)S(1)}, u32[]{:S(2)}, u32[]{:S(2)}) collective-permute-start(bf16[64,128]{1,0:T(8,128)(2,1)S(1)} %get-tuple-element.8), channel_id=1, source_target_pairs={{0,1},{1,0},{2,3},{3,2},{4,5},{5,4},{6,7},{7,6},{8,9},{9,8},{10,11... | collective-permute-start | bytes 49160 | tf_op jit(solution)/shard_map/ppermute | solution.py:292
  3.9 0.7 %reshape.17 = bf16[32,2,320]{2,1,0:T(2,128)(2,1)} reshape(bf16[32,10,64]{2,1,0:T(8,128)(2,1)S(1)} %all_to_all.7) | data formatting | bytes 81920
  4.6 6.9 %all-to-all-start = ((bf16[32,2,320]{2,1,0:T(2,128)(2,1)}), bf16[32,2,320]{2,1,0:T(2,128)(2,1)S(1)}, u32[]{:S(2)}, u32[]{:S(2)}) async-start(bf16[32,2,320]{2,1,0:T(2,128)(2,1)} %reshape.17), calls=%async_computation | async-start | bytes 98304 | tf_op jit(solution)/shard_map/all_to_all | solution.py:288
  11.5 0.0 collective-permute-done
  11.6 1.8 %collective-permute-start.1 = (bf16[64,256]{1,0:T(8,128)(2,1)S(1)}, bf16[64,256]{1,0:T(8,128)(2,1)S(1)}, u32[]{:S(2)}, u32[]{:S(2)}) collective-permute-start(bf16[64,256]{1,0:T(8,128)(2,1)S(1)} %pad_maximum_fusion.1), channel_id=1, source_target_pairs={{0,2},{1,3},{2,0},{3,1},{4,6},{5,7},{6,4},{7,5},{8,10},{9,11},{10,... | collective-permute-start | bytes 98312 | tf_op jit(solution)/shard_map/ppermute | solution.py:292
  13.4 0.0 copy-done.3
  13.4 0.0 copy-start.1
  13.4 1.5 %copy-done.1 = bf16[294,8,294]{2,1,0:T(8,128)(2,1)S(1)} copy-done((bf16[294,8,294]{2,1,0:T(8,128)(2,1)S(1)}, bf16[294,8,294]{2,1,0:T(8,128)(2,1)}, u32[]{:S(2)}) %copy-start.1) | copy-done | bytes 1383000
  14.9 0.8 %fold.1.down_ref = bf16[2352,64]{1,0:T(8,128)(2,1)S(1)} custom-call(bf16[64,294]{1,0:T(8,128)(2,1)S(1)} %bitcast.5, bf16[2352,294]{1,0:T(8,128)(2,1)S(1)} %bitcast.4), custom_call_target="tpu_custom_call" | custom-call | flops 500000000 | bytes 1 | tf_op jit(solution)/shard_map/fold/pallas_call | solution.py:306
  15.7 0.0 collective-permute-done.1
  15.7 0.0 copy-done.2
  15.7 0.0 copy-done
  15.7 3.7 %own.1.own_ref = f32[64,128]{1,0:T(8,128)S(1)} custom-call(s32[1,1]{1,0:T(1,128)} %bitcast.1.me_ref, s32[316,128]{1,0:T(8,128)S(1)} %copy-done.2, bf16[64,20224]{1,0:T(8,128)(2,1)S(1)} %copy-done, bf16[64,512]{1,0:T(8,128)(2,1)S(1)} %pad_maximum_fusion.pool_ref), custom_call_target="tpu_custom_call" | custom-call | flops 3000000000 | bytes 1 | tf_op jit(solution)/shard_map/own/pallas_call | solution.py:296
  19.4 0.0 all-to-all-done
  19.4 0.8 %reshape.18 = bf16[32,10,64]{2,1,0:T(8,128)(2,1)} reshape(bf16[32,2,320]{2,1,0:T(2,128)(2,1)S(1)} %all-to-all-done) | data formatting | bytes 81920
  20.2 0.9 %all_to_all.9.rows_ref = bf16[320,64]{1,0:T(8,128)(2,1)S(1)} reshape(bf16[32,10,64]{2,1,0:T(8,128)(2,1)} %reshape.18) | data formatting | bytes 81920 | tf_op jit(solution)/shard_map/all_to_all | solution.py:288
  21.1 4.9 %ghost_downward.1 = bf16[294,1024]{1,0:T(8,128)(2,1)} custom-call(s32[316,128]{1,0:T(8,128)S(1)} %copy-done.2, bf16[64,20224]{1,0:T(8,128)(2,1)S(1)} %copy-done, bf16[320,64]{1,0:T(8,128)(2,1)S(1)} %all_to_all.9.rows_ref, f32[64,128]{1,0:T(8,128)S(1)} %own.1.own_ref, bf16[2352,64]{1,0:T(8,128)(2,1)S(1)} %fold.1.down_ref), custom_call_target="tpu_custom_call" | custom-call | tf_op jit(solution)/shard_map/ghost_downward/pallas_call | solution.py:317
  (4 shorter events, 0.1 us)
Async XLA Ops:
  0.0 13.4 %copy-start.3 = (bf16[294,64]{0,1:T(8,128)(2,1)S(1)}, bf16[294,64]{0,1:T(8,128)(2,1)}, u32[]{:S(2)}) copy-start(bf16[294,64]{0,1:T(8,128)(2,1)} %param.12) | copy-start | bytes 112900
  0.0 15.7 %copy-start.2 = (s32[316,128]{1,0:T(8,128)S(1)}, s32[316,128]{1,0:T(8,128)}, u32[]{:S(2)}) copy-start(s32[316,128]{1,0:T(8,128)} %list_ref.3) | copy-start | bytes 485380
  3.2 12.5 %copy-start = (bf16[64,20224]{1,0:T(8,128)(2,1)S(1)}, bf16[64,20224]{1,0:T(8,128)(2,1)}, u32[]{:S(2)}) copy-start(bf16[64,20224]{1,0:T(8,128)(2,1)} %matrix_ref.3) | copy-start | bytes 7766020
  3.2 8.3 %collective-permute-start = (bf16[64,128]{1,0:T(8,128)(2,1)S(1)}, bf16[64,128]{1,0:T(8,128)(2,1)S(1)}, u32[]{:S(2)}, u32[]{:S(2)}) collective-permute-start(bf16[64,128]{1,0:T(8,128)(2,1)S(1)} %get-tuple-element.8), channel_id=1, source_target_pairs={{0,1},{1,0},{2,3},{3,2},{4,5},{5,4},{6,7},{7,6},{8,9},{9,8},{10,11... | collective-permute-start | bytes 49160 | tf_op jit(solution)/shard_map/ppermute | solution.py:292
  4.6 14.8 %all-to-all-start = ((bf16[32,2,320]{2,1,0:T(2,128)(2,1)}), bf16[32,2,320]{2,1,0:T(2,128)(2,1)S(1)}, u32[]{:S(2)}, u32[]{:S(2)}) async-start(bf16[32,2,320]{2,1,0:T(2,128)(2,1)} %reshape.17), calls=%async_computation | async-start | bytes 98304 | tf_op jit(solution)/shard_map/all_to_all | solution.py:288
  11.6 4.1 %collective-permute-start.1 = (bf16[64,256]{1,0:T(8,128)(2,1)S(1)}, bf16[64,256]{1,0:T(8,128)(2,1)S(1)}, u32[]{:S(2)}, u32[]{:S(2)}) collective-permute-start(bf16[64,256]{1,0:T(8,128)(2,1)S(1)} %pad_maximum_fusion.1), channel_id=1, source_target_pairs={{0,2},{1,3},{2,0},{3,1},{4,6},{5,7},{6,4},{7,5},{8,10},{9,11},{10,... | collective-permute-start | bytes 98312 | tf_op jit(solution)/shard_map/ppermute | solution.py:292
  13.4 1.5 %copy-start.1 = (bf16[294,8,294]{2,1,0:T(8,128)(2,1)S(1)}, bf16[294,8,294]{2,1,0:T(8,128)(2,1)}, u32[]{:S(2)}) copy-start(bf16[294,8,294]{2,1,0:T(8,128)(2,1)} %param.13) | copy-start | bytes 4148932

commit v3 on v2

--- a/solution.py
+++ b/solution.py
@@ -8,6 +8,7 @@
 from jax.sharding import PartitionSpec as P
 
 LANES = 128
+ROWS = 8
 VMEM = pl.BlockSpec(memory_space=pltpu.VMEM)
 HBM = pl.BlockSpec(memory_space=pltpu.HBM)
 SMEM = pl.BlockSpec(memory_space=pltpu.SMEM)
@@ -34,7 +35,10 @@
     return [(at, min(size, total - at)) for at in range(0, total, size)]
 
 
-def upward_kernel(x_hbm, u_hbm, p_hbm, map_hbm, packed_ref, ghost_ref, x_ref, u_ref, p_ref, map_ref, slots, wide, parent, sems):
+def upward_kernel(
+    groups, x_hbm, u_hbm, p_hbm, map_hbm, packed_ref, ghost_ref,
+    x_ref, u_ref, p_ref, map_ref, slots, wide, parent, taken_rows, sems
+):
     surface = x_ref.shape[0]
     coeff = p_ref.shape[0]
     used = map_hbm.shape[1]
@@ -83,9 +87,16 @@
         ids = jnp.broadcast_to(slots[:, at : at + LANES], (coeff, LANES))
         taken = lane_gather(packed, (ids & (LANES - 1)).astype(jnp.int16)).astype(jnp.float32)
         taken = jnp.where(ids < LANES, taken, 0.0)
-        rows = jnp.transpose(taken).astype(jnp.bfloat16)
-        keep = min(LANES, used - at)
-        ghost_ref[at : at + keep, :] = rows[:keep, :]
+        taken_rows[at : at + LANES, :] = jnp.transpose(taken)
+    width = used // groups
+    copies = ghost_ref.shape[0] // (groups * ROWS)
+    for g in range(groups):
+        first = taken_rows[g * width : g * width + ROWS, :]
+        second = taken_rows[g * width + ROWS : g * width + 2 * ROWS, :]
+        rows = jnp.concatenate([first, second], axis=1).astype(jnp.bfloat16)
+        for n in range(copies):
+            at = (n * groups + g) * ROWS
+            ghost_ref[at : at + ROWS, :] = rows
 
 
 def spread(row, rows):
@@ -200,30 +211,50 @@
     ]
 
 
-def own_kernel(me_ref, list_ref, matrix_ref, pool_ref, out_ref, code, stack, picked):
+def own_kernel(
+    me_ref, list_ref, matrix_ref, pool_ref, e_ref, d_hbm, out_ref, down_ref, code, stack, picked, d_ref, sem
+):
+    d_copy = pltpu.make_async_copy(d_hbm, d_ref, sem)
+    d_copy.start()
     me = me_ref[0, 0]
     lists = list_ref[...]
     code[...] = jnp.where(lists < pool_ref.shape[1], lists ^ (me * LANES), -1)
     out_ref[...] = translate(code, matrix_ref, pool_ref, stack, picked)
-
-
-def fold_kernel(e_ref, d_ref, down_ref):
+    d_copy.wait()
     down_ref[...] = lax.dot_general(
         d_ref[...], e_ref[...], (((1,), (1,)), ((), ())), preferred_element_type=jnp.float32
     ).astype(jnp.bfloat16)
 
 
-def ghost_kernel(own_boxes, list_ref, matrix_ref, rows_ref, own_ref, down_ref, out_ref, code, stack, picked, pool, wide):
+def ghost_kernel(
+    own_boxes, width, list_ref, matrix_ref, rows_ref, own_ref, down_ref, out_ref, code, stack, picked, pool, extra, wide
+):
     coeff = matrix_ref.shape[0]
     surface = out_ref.shape[0]
-    slots = rows_ref.shape[0]
+    lanes = rows_ref.shape[0]
+    senders = lanes // ROWS
+    more = width - ROWS
     lists = list_ref[...] - own_boxes
-    code[...] = jnp.where(lists < slots, lists, -1)
-    for at, size in chunks_of(slots, LANES):
-        rows = rows_ref[at : at + size, :].astype(jnp.float32)
-        if size < LANES:
-            rows = jnp.concatenate([rows, jnp.zeros((LANES - size, coeff), jnp.float32)], axis=0)
-        pool[:, at : at + LANES] = jnp.transpose(rows).astype(jnp.bfloat16)
+    sender = ((lists.astype(jnp.float32) + 0.5) * (1.0 / width)).astype(jnp.int32)
+    slot = lists - sender * width
+    place = jnp.where(
+        slot < ROWS, sender * ROWS + slot, lanes + sender * more + slot - ROWS
+    )
+    code[...] = jnp.where((lists >= 0) & (lists < senders * width), place, -1)
+    for at in range(0, lanes, LANES):
+        turned = jnp.transpose(rows_ref[at : at + LANES, :].astype(jnp.float32)).astype(jnp.bfloat16)
+        pool[:, at : at + LANES] = turned[0:coeff, :]
+        extra[:, at : at + LANES] = turned[coeff : 2 * coeff, :]
+    for at in range(0, pool.shape[1] - lanes, LANES):
+        m = lax.broadcasted_iota(jnp.int32, (coeff, LANES), 1) + at
+        source = (m >> (more.bit_length() - 1)) * ROWS + (m & (more - 1))
+        lane, tile = (source & (LANES - 1)).astype(jnp.int16), (source >> 7).astype(jnp.int16)
+        got = jnp.zeros((coeff, LANES), jnp.bfloat16)
+        first = at // more * ROWS // LANES
+        for k in range(first, min(first + LANES // more * ROWS // LANES, lanes // LANES)):
+            part = lane_gather(extra[:, k * LANES : (k + 1) * LANES], lane)
+            got = jnp.where(tile == jnp.int16(k), part, got)
+        pool[:, lanes + at : lanes + at + LANES] = got
     total = translate(code, matrix_ref, pool, stack, picked)
     local_coeff = (total + own_ref[...]).astype(jnp.bfloat16)
     for at, size in chunks_of(surface, 96):
@@ -255,13 +286,17 @@
     sub_count = lax.axis_size("sub")
     if boxes != LANES or sub_count & (sub_count - 1):
         raise ValueError("unsupported sizes")
-    slot_lanes = -(-slots // LANES) * LANES
+    slot_lanes = -(-(slots + ROWS) // LANES) * LANES
+    width = slots // grp_count
+    more = width - ROWS
+    if 2 * coeff != LANES or not 0 < more <= ROWS or more & (more - 1):
+        raise ValueError("unsupported sizes")
     lane_tiles = -(-surface // LANES)
-    packed, ghosts = pl.pallas_call(
-        upward_kernel,
+    packed, send = pl.pallas_call(
+        functools.partial(upward_kernel, grp_count),
         out_shape=(
             jax.ShapeDtypeStruct((coeff, boxes), jnp.bfloat16),
-            jax.ShapeDtypeStruct((slots, coeff), jnp.bfloat16),
+            jax.ShapeDtypeStruct((sub_count * grp_count * ROWS, LANES), jnp.bfloat16),
         ),
         in_specs=[HBM] * 4,
         out_specs=(VMEM, VMEM),
@@ -273,6 +308,7 @@
             pltpu.VMEM((1, slot_lanes), jnp.int32),
             pltpu.VMEM((lane_tiles, surface * 8, LANES), jnp.float32),
             pltpu.VMEM((surface, boxes), jnp.bfloat16),
+            pltpu.VMEM((slot_lanes, coeff), jnp.float32),
             pltpu.SemaphoreType.DMA((3 + len(chunks_of(surface, 96)),)),
         ],
         compiler_params=pltpu.CompilerParams(vmem_limit_bytes=40000 << 10),
@@ -281,10 +317,14 @@
     )(
         *(
             pltpu.with_memory_space_constraint(a, pltpu.HBM)
-            for a in (child_moments, upward_matrix.reshape(surface * 8, surface), project_matrix, ghost_map)
+            for a in (
+                child_moments,
+                upward_matrix.reshape(surface * 8, surface),
+                project_matrix,
+                ghost_map,
+            )
         )
     )
-    send = jnp.broadcast_to(ghosts[None], (sub_count, slots, coeff)).reshape(sub_count * slots, coeff)
     received = lax.all_to_all(send, ("sub", "grp"), split_axis=0, concat_axis=0, tiled=True)
     own = packed
     hop = 1
@@ -293,35 +333,41 @@
         own = jnp.concatenate([own, other], axis=1)
         hop *= 2
     me = lax.axis_index("sub").astype(jnp.int32).reshape(1, 1)
-    own_part = pl.pallas_call(
+    own_part, down = pl.pallas_call(
         own_kernel,
-        out_shape=jax.ShapeDtypeStruct((coeff, boxes), jnp.float32),
-        in_specs=[SMEM] + [VMEM] * 3,
-        out_specs=VMEM,
-        scratch_shapes=translate_scratch(offsets, coeff, own.shape[1]),
-        compiler_params=pltpu.CompilerParams(vmem_limit_bytes=20 << 20),
+        out_shape=(
+            jax.ShapeDtypeStruct((coeff, boxes), jnp.float32),
+            jax.ShapeDtypeStruct((surface * 8, coeff), jnp.bfloat16),
+        ),
+        in_specs=[SMEM] + [VMEM] * 4 + [HBM],
+        out_specs=(VMEM, VMEM),
+        scratch_shapes=translate_scratch(offsets, coeff, own.shape[1])
+        + [
+            pltpu.VMEM((surface * 8, surface), jnp.bfloat16),
+            pltpu.SemaphoreType.DMA(()),
+        ],
+        compiler_params=pltpu.CompilerParams(vmem_limit_bytes=24 << 20),
         cost_estimate=pl.CostEstimate(flops=3_000_000_000, bytes_accessed=1, transcendentals=0),
         name="own",
-    )(me, neighbour_list, transfer_matrix, own)
-    down = pl.pallas_call(
-        fold_kernel,
-        out_shape=jax.ShapeDtypeStruct((surface * 8, coeff), jnp.bfloat16),
-        in_specs=[VMEM] * 2,
-        out_specs=VMEM,
-        compiler_params=pltpu.CompilerParams(vmem_limit_bytes=8 << 20),
-        cost_estimate=pl.CostEstimate(flops=500_000_000, bytes_accessed=1, transcendentals=0),
-        name="fold",
-    )(jnp.transpose(expand_matrix), downward_matrix.reshape(surface * 8, surface))
-    ghost_count = received.shape[0]
-    ghost_lanes = -(-ghost_count // LANES) * LANES
+    )(
+        me,
+        neighbour_list,
+        transfer_matrix,
+        own,
+        jnp.transpose(expand_matrix),
+        pltpu.with_memory_space_constraint(downward_matrix.reshape(surface * 8, surface), pltpu.HBM),
+    )
+    sent_lanes = received.shape[0]
+    ghost_lanes = sent_lanes + -(-(sent_lanes // ROWS * more) // LANES) * LANES
     result = pl.pallas_call(
-        functools.partial(ghost_kernel, sub_count * boxes),
+        functools.partial(ghost_kernel, sub_count * boxes, width),
         out_shape=jax.ShapeDtypeStruct((surface, 8 * boxes), jnp.bfloat16),
         in_specs=[VMEM] * 5,
         out_specs=VMEM,
         scratch_shapes=translate_scratch(offsets, coeff, ghost_lanes)
         + [
             pltpu.VMEM((coeff, ghost_lanes), jnp.bfloat16),
+            pltpu.VMEM((coeff, sent_lanes), jnp.bfloat16),
             pltpu.VMEM((surface * 8, boxes), jnp.float32),
         ],
         compiler_params=pltpu.CompilerParams(vmem_limit_bytes=20 << 20),

time: 26.2 us -> 25.6 us (0.977)
  local copies, waits for them, and re-layouts: 4.02 us -> 0.01 us
  waiting for transfers between devices: 0.01 us -> 3.51 us
  Pallas kernels: 12.5 us -> 13.6 us
  starting transfers between devices: 9.34 us -> 8.3 us
    unnamed x10 -> x6, local copies, waits for them, and re-layouts: 3.02 us -> 0.01 us
    all_to_all x1, waiting for transfers between devices: 0.01 us -> 2.67 us  [on_device(): lax.all_to_all(send, ('sub', 'grp'), split_axis=0, concat_axis=0, tiled=T...]
    all_to_all x1, starting transfers between devices: 6.95 us -> 4.89 us  [on_device(): lax.all_to_all(send, ('sub', 'grp'), split_axis=0, concat_axis=0, tiled=T...]
    pallas_call x4 -> x3, Pallas kernels: 12.5 us -> 13.6 us  [the longest x1 4.98 us: on_device(): pl.pallas_call(functools.partial(ghost_kernel, sub_count * boxes, width),...]
    ppermute x2, starting transfers between devices: 2.39 us -> 3.41 us  [on_device(): other = lax.ppermute(own, 'sub', [(i, i ^ hop) for i in range(sub_count)])]
    all_to_all x2 -> x0, local copies, waits for them, and re-layouts: 0.98 us -> none  [on_device(): lax.all_to_all(send, ('sub', 'grp'), split_axis=0, concat_axis=0, tiled=T...]
    ppermute x2, waiting for transfers between devices: 0.01 us -> 0.84 us  [on_device(): other = lax.ppermute(own, 'sub', [(i, i ^ hop) for i in range(sub_count)])]
  transfers between devices with their start and end apart: 3 -> 3, of which waited for: 0 -> 2; matrix products, arithmetic and copies ran while one was open for 3% -> 0% of each run, Pallas kernels for 17% -> 18%
where the time goes in v3:
time: 25.6 us; the launch traced here: 25.5 us
  Pallas kernels  13.6 us (53%)
  starting transfers between devices  8.3 us (32%)
  waiting for transfers between devices  3.51 us (14%)
    pallas_call x1, Pallas kernels, on_device(): pl.pallas_call(functools.partial(ghost_kernel, sub_count * boxes, width),...  4.98 us
    all_to_all x1, starting transfers between devices, on_device(): lax.all_to_all(send, ('sub', 'grp'), split_axis=0, concat_axis=0, tiled=T...  4.89 us
    pallas_call x1, Pallas kernels, on_device(): pl.pallas_call(own_kernel, out_shape=(jax.ShapeDtypeStruct((coeff, boxes)...  4.53 us
    pallas_call x1, Pallas kernels, on_device(): pl.pallas_call(functools.partial(upward_kernel, grp_count), out_shape=(ja...  4.04 us
    ppermute x2, starting transfers between devices, on_device(): other = lax.ppermute(own, 'sub', [(i, i ^ hop) for i in range(sub_count)])  3.41 us
    all_to_all x1, waiting for transfers between devices, on_device(): lax.all_to_all(send, ('sub', 'grp'), split_axis=0, concat_axis=0, tiled=T...  2.67 us
    ppermute x2, waiting for transfers between devices, on_device(): other = lax.ppermute(own, 'sub', [(i, i ^ hop) for i in range(sub_count)])  0.84 us
  transfers between devices with their start and end apart: 3, of which 2 were waited for; matrix products, arithmetic and copies ran while one was open for 0% of the time, Pallas kernels for 18%

profile of v3, /device:TPU:0, one launch (start us, length us, event | category | flops | bytes accessed | tf_op | source)
XLA Modules:
  0.0 25.5 jit_solution(14361763859676754254)
XLA Ops:
  0.0 0.0 copy-start.1
  0.0 0.0 copy-start
  0.0 0.0 copy-start.2
  0.0 4.0 %upward.1 = (bf16[64,128]{1,0:T(8,128)(2,1)S(1)}, bf16[256,128]{1,0:T(8,128)(2,1)}) custom-call(bf16[294,1024]{1,0:T(8,128)(2,1)} %x_hbm.1, bf16[2352,294]{1,0:T(8,128)(2,1)} %bitcast.8, bf16[64,294]{1,0:T(8,128)(2,1)} %p_hbm.1, s32[1,80]{1,0:T(1,128)} %map_hbm.1), custom_call_target="tpu_custom_call" | custom-call | flops 500000000 | bytes 3000000 | tf_op jit(solution)/shard_map/upward/pallas_call | solution.py:295
  4.1 0.6 %collective-permute-start = (bf16[64,128]{1,0:T(8,128)(2,1)S(1)}, bf16[64,128]{1,0:T(8,128)(2,1)S(1)}, u32[]{:S(2)}, u32[]{:S(2)}) collective-permute-start(bf16[64,128]{1,0:T(8,128)(2,1)S(1)} %get-tuple-element.10), channel_id=1, source_target_pairs={{0,1},{1,0},{2,3},{3,2},{4,5},{5,4},{6,7},{7,6},{8,9},{9,8},{10,11... | collective-permute-start | bytes 49160 | tf_op jit(solution)/shard_map/ppermute | solution.py:332
  4.6 0.8 %collective-permute-done = bf16[64,128]{1,0:T(8,128)(2,1)S(1)} collective-permute-done((bf16[64,128]{1,0:T(8,128)(2,1)S(1)}, bf16[64,128]{1,0:T(8,128)(2,1)S(1)}, u32[]{:S(2)}, u32[]{:S(2)}) %collective-permute-start) | collective-permute-done | bytes 16416 | tf_op jit(solution)/shard_map/ppermute | solution.py:332
  5.5 2.8 %collective-permute-start.1 = (bf16[64,256]{1,0:T(8,128)(2,1)S(1)}, bf16[64,256]{1,0:T(8,128)(2,1)S(1)}, u32[]{:S(2)}, u32[]{:S(2)}) collective-permute-start(bf16[64,256]{1,0:T(8,128)(2,1)S(1)} %pad_maximum_fusion.1), channel_id=1, source_target_pairs={{0,2},{1,3},{2,0},{3,1},{4,6},{5,7},{6,4},{7,5},{8,10},{9,11},{10,... | collective-permute-start | bytes 98312 | tf_op jit(solution)/shard_map/ppermute | solution.py:332
  8.3 4.9 %all-to-all-start = ((bf16[32,8,128]{2,1,0:T(8,128)(2,1)}), bf16[32,8,128]{2,1,0:T(8,128)(2,1)S(1)}, u32[]{:S(2)}, u32[]{:S(2)}) async-start(bf16[32,8,128]{2,1,0:T(8,128)(2,1)} %bitcast.1), calls=%async_computation | async-start | bytes 131072 | tf_op jit(solution)/shard_map/all_to_all | solution.py:328
  13.2 0.0 collective-permute-done.1
  13.2 0.0 copy-done.1
  13.3 0.0 copy-done
  13.3 0.0 copy-done.2
  13.3 4.5 %own.1 = (f32[64,128]{1,0:T(8,128)S(1)}, bf16[2352,64]{1,0:T(8,128)(2,1)S(1)}) custom-call(s32[1,1]{1,0:T(1,128)} %bitcast.3.me_ref, s32[316,128]{1,0:T(8,128)S(1)} %copy-done.1, bf16[64,20224]{1,0:T(8,128)(2,1)S(1)} %copy-done, bf16[64,512]{1,0:T(8,128)(2,1)S(1)} %pad_maximum_fusion.pool_ref, bf16[64,294]{1,0:T(8,128)(2,1)S(1)} %bitcast.7, ...), custom_call_target="tpu_custom_call" | custom-call | flops 3000000000 | bytes 1 | tf_op jit(solution)/shard_map/own/pallas_call | solution.py:336
  17.8 2.7 %all-to-all-done = bf16[32,8,128]{2,1,0:T(8,128)(2,1)S(1)} async-done(((bf16[32,8,128]{2,1,0:T(8,128)(2,1)}), bf16[32,8,128]{2,1,0:T(8,128)(2,1)S(1)}, u32[]{:S(2)}, u32[]{:S(2)}) %all-to-all-start) | async-done | bytes 65568 | tf_op jit(solution)/shard_map/all_to_all | solution.py:328
  20.5 5.0 %ghost_downward.1 = bf16[294,1024]{1,0:T(8,128)(2,1)} custom-call(s32[316,128]{1,0:T(8,128)S(1)} %copy-done.1, bf16[64,20224]{1,0:T(8,128)(2,1)S(1)} %copy-done, bf16[256,128]{1,0:T(8,128)(2,1)S(1)} %bitcast.6, f32[64,128]{1,0:T(8,128)S(1)} %get-tuple-element.11.own_ref, bf16[2352,64]{1,0:T(8,128)(2,1)S(1)} %get-tuple-element.12.down_ref), custom_call_target="tpu_custom_call" | custom-call | tf_op jit(solution)/shard_map/ghost_downward/pallas_call | solution.py:362
  (2 shorter events, 0.0 us)
Async XLA Ops:
  0.0 13.2 %copy-start.1 = (s32[316,128]{1,0:T(8,128)S(1)}, s32[316,128]{1,0:T(8,128)}, u32[]{:S(2)}) copy-start(s32[316,128]{1,0:T(8,128)} %list_ref.3) | copy-start | bytes 485380
  0.0 13.3 %copy-start = (bf16[64,20224]{1,0:T(8,128)(2,1)S(1)}, bf16[64,20224]{1,0:T(8,128)(2,1)}, u32[]{:S(2)}) copy-start(bf16[64,20224]{1,0:T(8,128)(2,1)} %matrix_ref.3) | copy-start | bytes 7766020
  0.0 13.3 %copy-start.2 = (bf16[294,64]{0,1:T(8,128)(2,1)S(1)}, bf16[294,64]{0,1:T(8,128)(2,1)}, u32[]{:S(2)}) copy-start(bf16[294,64]{0,1:T(8,128)(2,1)} %param.12) | copy-start | bytes 112900
  4.1 1.4 %collective-permute-start = (bf16[64,128]{1,0:T(8,128)(2,1)S(1)}, bf16[64,128]{1,0:T(8,128)(2,1)S(1)}, u32[]{:S(2)}, u32[]{:S(2)}) collective-permute-start(bf16[64,128]{1,0:T(8,128)(2,1)S(1)} %get-tuple-element.10), channel_id=1, source_target_pairs={{0,1},{1,0},{2,3},{3,2},{4,5},{5,4},{6,7},{7,6},{8,9},{9,8},{10,11... | collective-permute-start | bytes 49160 | tf_op jit(solution)/shard_map/ppermute | solution.py:332
  5.5 7.8 %collective-permute-start.1 = (bf16[64,256]{1,0:T(8,128)(2,1)S(1)}, bf16[64,256]{1,0:T(8,128)(2,1)S(1)}, u32[]{:S(2)}, u32[]{:S(2)}) collective-permute-start(bf16[64,256]{1,0:T(8,128)(2,1)S(1)} %pad_maximum_fusion.1), channel_id=1, source_target_pairs={{0,2},{1,3},{2,0},{3,1},{4,6},{5,7},{6,4},{7,5},{8,10},{9,11},{10,... | collective-permute-start | bytes 98312 | tf_op jit(solution)/shard_map/ppermute | solution.py:332
  8.3 12.2 %all-to-all-start = ((bf16[32,8,128]{2,1,0:T(8,128)(2,1)}), bf16[32,8,128]{2,1,0:T(8,128)(2,1)S(1)}, u32[]{:S(2)}, u32[]{:S(2)}) async-start(bf16[32,8,128]{2,1,0:T(8,128)(2,1)} %bitcast.1), calls=%async_computation | async-start | bytes 131072 | tf_op jit(solution)/shard_map/all_to_all | solution.py:328
